TPU v7x, 16 devices: a whole 2x2x2 slice. The times are simulated.
16 devices in a mesh: dp: 16 (over z, y, x, core).
Axes of the slice: x: 2, y: 2, z: 2, core: 2. Of those that a mesh axis runs over, the one named last changes fastest.
Arguments:
- x_embed: bfloat16 [4096, 512], P('dp')
- positions: int32 [4096], P('dp')
- k_cache: bfloat16 [2, 4096, 32, 8, 64], P(None, 'dp')
- v_cache: bfloat16 [2, 4096, 32, 8, 64], P(None, 'dp')
- ln1_gain: bfloat16 [2, 512], P(None, 'dp')
- ln1_bias: bfloat16 [2, 512], P(None, 'dp')
- ln2_gain: bfloat16 [2, 512], P(None, 'dp')
- ln2_bias: bfloat16 [2, 512], P(None, 'dp')
- w_qkv: bfloat16 [2, 512, 1536], P(None, 'dp')
- b_qkv: bfloat16 [2, 1536], P(None, 'dp')
- w_out: bfloat16 [2, 512, 512], P(None, 'dp')
- b_out: bfloat16 [2, 512], P(None, 'dp')
- w_in: bfloat16 [2, 512, 2048], P(None, 'dp')
- b_in: bfloat16 [2, 2048], P(None, 'dp')
- w_down: bfloat16 [2, 2048, 512], P(None, 'dp')
- b_down: bfloat16 [2, 512], P(None, 'dp')
- lnf_gain: bfloat16 [512], P('dp')
- lnf_bias: bfloat16 [512], P('dp')
Outputs:
- output 1: bfloat16 [4096, 512], P('dp')
- output 2: bfloat16 [2, 4096, 32, 8, 64], P(None, 'dp')
- output 3: bfloat16 [2, 4096, 32, 8, 64], P(None, 'dp')
All inputs are finite; a program needn't handle non-finite values.
Results may differ from a plain program's by a relative error of at most 0.0104128.
Values are sent between devices in bfloat16 or wider.
A program may use at most 1 GiB of HBM per device.

v0:
```python
import math

import jax
import jax.numpy as jnp
from jax import lax
from jax.experimental import pallas as pl
from jax.experimental.pallas import tpu as pltpu
from jax.sharding import PartitionSpec as P

LN_EPS = 1e-5
ROPE_BASE = 10000.0
F32 = jnp.float32
BF16 = jnp.bfloat16
MESH = pl.DeviceIdType.MESH
GRID = (2,) * 5

ERF_NUM = (-2.72614225801306e-10, 2.77068142495902e-08, -2.10102402082508e-06,
           -5.69250639462346e-05, -7.34990630326855e-04, -2.95459980854025e-03,
           -1.60960333262415e-02)
ERF_DEN = (-1.45660718464996e-05, -2.13374055278905e-04, -1.68282697438203e-03,
           -7.37332916720468e-03, -1.42647390514189e-02)


def horner(coefs, t):
    acc = jnp.full_like(t, coefs[0])
    for coef in coefs[1:]:
        acc = acc * t + coef
    return acc


def gelu(v):
    u = jnp.clip(v * (0.5 ** 0.5), -4.0, 4.0)
    t = u * u
    erf = u * horner(ERF_NUM, t) / horner(ERF_DEN, t)
    return 0.5 * v * (1.0 + erf)


def normalize(v):
    centered = v - jnp.mean(v, axis=-1, keepdims=True)
    var = jnp.mean(centered * centered, axis=-1, keepdims=True)
    return centered * lax.rsqrt(var + LN_EPS)


QO = ((0, (0, 32), (0, 640), 0), (0, (0, 32), (640, 640), 1),
      (0, (0, 32), (1280, 256), 2), (1, (0, 32), (0, 512), 2))
IN = ((2, (0, 32), (0, 640), 0), (2, (0, 32), (640, 640), 1), (2, (0, 32), (1280, 768), 2))
DOWN = ((3, (0, 48), (0, 512), 0), (3, (48, 48), (0, 512), 1), (3, (96, 32), (0, 512), 2))
PIECES = (
    [(m, 0, r, c, o) for m, r, c, o in QO] + [(4, 0, (0, 8), (0, 128), 0)],
    [(m, 0, r, c, o) for m, r, c, o in IN],
    [(m, 0, r, c, o) for m, r, c, o in DOWN],
    [(m, 1, r, c, o) for m, r, c, o in QO],
    [(m, 1, r, c, o) for m, r, c, o in IN],
    [(m, 1, r, c, o) for m, r, c, o in DOWN],
)
ITEMS = [it for piece in PIECES for it in piece]
N_ITEMS = len(ITEMS)


def kernel(x_ref, pos_ref, vec_in, wq_in, wo_in, wi_in, wd_in, kc_in, vc_in,
           out_ref, ko_ref, vo_ref,
           wq, wo, wi, wd, vecs,
           lnp, bqkv, bin_, qs, kn, vn, sc, pr, ctxt, hcur, h2s, act, accr,
           posb, local_sem, cache_sem, send_sem, recv_sem):
    me = lax.axis_index('dp')
    core = me % 2
    px = (me // 2) % 2
    py = (me // 4) % 2
    pz = me // 8
    peer_core = me + 1 - 2 * core
    peers = (me + 2 - 4 * px, me + 4 - 8 * py, me + 8 - 16 * pz)
    mats = (wq, wo, wi, wd, vecs)
    shards = (wq_in, wo_in, wi_in, wd_in, vec_in)

    local = {}
    order = [(m, l) for l in range(2) for m in (0, 1, 4, 2, 3) if m != 4 or l == 0]
    for i, (m, l) in enumerate(order):
        src = shards[m].at[l] if m != 4 else shards[m]
        local[(m, l)] = pltpu.make_async_copy(
            src, mats[m].at[l, pz, py, px, core], local_sem.at[i])
        local[(m, l)].start()

    barrier = pltpu.get_barrier_semaphore()
    for peer in peers + (peer_core,):
        pl.semaphore_signal(barrier, inc=1, device_id=(peer,), device_id_type=MESH)
    pl.semaphore_wait(barrier, 4)

    def view(item, full):
        m, l, (r0, rn), (c0, cn), _ = item
        at = [slice(None) if ax in full else v for ax, v in ((2, pz), (1, py), (0, px))]
        return mats[m].at[(l, *at, core, pl.ds(r0, rn), pl.ds(c0, cn))]

    sends = {}

    def send(i, stage):
        item = ITEMS[i]
        o = item[4]
        axes = [(o + s) % 3 for s in range(3)]
        if stage < 3:
            ref = view(item, axes[:stage])
            peer = peers[axes[stage]]
        else:
            if stage == 3:
                ref = view(item, axes[:2])
            else:
                m, l, (r0, rn), (c0, cn), _ = item
                own = (px, py, pz)[axes[2]]
                at = [slice(None), slice(None), slice(None)]
                at[2 - axes[2]] = 1 - own
                ref = mats[m].at[(l, *at, core, pl.ds(r0, rn), pl.ds(c0, cn))]
            peer = peer_core
        copy = pltpu.make_async_remote_copy(
            src_ref=ref, dst_ref=ref, send_sem=send_sem.at[i, stage],
            recv_sem=recv_sem.at[i, stage], device_id=(peer,), device_id_type=MESH)
        copy.start()
        sends[(i, stage)] = copy

    starts = [0]
    for piece in PIECES:
        starts.append(starts[-1] + len(piece))

    def ids(p):
        return range(starts[p], starts[p + 1])

    waited = set()

    def a(p):
        for i in ids(p):
            key = (ITEMS[i][0], ITEMS[i][1])
            if key not in waited:
                waited.add(key)
                local[key].wait()
        for i in ids(p):
            send(i, 0)

    def b(p):
        for i in ids(p):
            sends[(i, 0)].wait_recv()
            send(i, 1)

    def c(p):
        for i in ids(p):
            sends[(i, 1)].wait_recv()
            send(i, 2)
            send(i, 3)

    def d(p):
        for i in ids(p):
            sends[(i, 2)].wait_recv()
            send(i, 4)

    def e(p):
        for i in ids(p):
            sends[(i, 3)].wait_recv()
            sends[(i, 4)].wait_recv()

    a(0)
    a(1)
    a(2)
    cache = []
    for l in range(2):
        for j, (src, dst) in enumerate(((kc_in, ko_ref), (vc_in, vo_ref))):
            cp = pltpu.make_async_copy(src.at[l], dst.at[l], cache_sem.at[2 * l + j])
            cp.start()
            cache.append(cp)

    pos = pos_ref[...]
    posf = pos.astype(F32)
    posb[...] = jnp.broadcast_to(posf, (16, 256)).astype(BF16)
    row8 = lax.broadcasted_iota(jnp.int32, (8, 256), 0)
    inv_freq = jnp.full((8, 256), 1.0, F32)
    for i in range(1, 8):
        inv_freq = jnp.where(row8 == i, F32(ROPE_BASE ** (-i / 8.0)), inv_freq)
    angle = jnp.broadcast_to(posf, (8, 256)) * inv_freq
    cos_t = jnp.cos(angle)
    sin_t = jnp.sin(angle)
    hcur[...] = x_ref[...]

    b(0)
    b(1)
    c(0)
    a(3)
    b(2)
    d(0)
    c(1)
    e(0)
    a(4)
    b(3)

    vall = vecs[...].reshape(16, 8, 128).astype(F32)
    lane128 = lax.broadcasted_iota(jnp.int32, (128, 512), 0)
    lane512 = lax.broadcasted_iota(jnp.int32, (128, 512), 1)
    spread = jnp.where(lane128 % 32 == lane512 % 32, 1.0, 0.0).astype(BF16)
    dev_row = lax.broadcasted_iota(jnp.int32, (16, 512), 0)
    own = lax.broadcasted_iota(jnp.int32, (16, 512), 1) // 32 == dev_row
    quarter = lax.broadcasted_iota(jnp.int32, (16, 128), 1) // 32
    qa = lax.broadcasted_iota(jnp.int32, (128, 1536), 0)
    qn = lax.broadcasted_iota(jnp.int32, (128, 1536), 1)
    spread_q = jnp.where(qa == qn % 96, 1.0, 0.0).astype(BF16)
    own_q = (lax.broadcasted_iota(jnp.int32, (16, 1536), 1) // 96
             == lax.broadcasted_iota(jnp.int32, (16, 1536), 0))
    for l in range(2):
        for half in range(2):
            share = vall[:, 4 * l + half, :]
            for k in range(4 if half == 0 else 3):
                part = jnp.where(quarter == k, share, 0.0).astype(BF16)
                wide = jnp.dot(part, spread, preferred_element_type=F32)
                lnp[l, 4 * half + k] = jnp.sum(jnp.where(own, wide, 0.0), axis=0, keepdims=True)
        wide = jnp.dot(vall[:, 4 * l + 2, :].astype(BF16), spread_q, preferred_element_type=F32)
        bqkv[l] = jnp.sum(jnp.where(own_q, wide, 0.0), axis=0, keepdims=True)
        share = vall[:, 4 * l + 3, :]
        for n in range(8):
            bin_[l, n] = jnp.concatenate([share[2 * n:2 * n + 1], share[2 * n + 1:2 * n + 2]], axis=1)

    def rope(t):
        r1, r2 = t[0:8], t[8:16]
        rot = jnp.concatenate([r1 * cos_t - r2 * sin_t, r2 * cos_t + r1 * sin_t, t[16:]], axis=0)
        return rot.astype(BF16)

    def qkv_stage(l):
        normed = normalize(hcur[...].astype(F32))
        h1 = (normed * lnp[l, 0] + lnp[l, 1]).astype(BF16)
        h2s[...] = (normed * lnp[l, 2] + lnp[l, 3]).astype(BF16)
        for j in range(4):
            w = wq[l, :, :, :, :, :, pl.ds(384 * j, 384)].reshape(512, 384)
            y = jnp.dot(h1, w, preferred_element_type=F32) + bqkv[l][:, 384 * j:384 * (j + 1)]
            yt = y.astype(BF16).astype(F32).T
            for g in range(2):
                base = 192 * g
                qs[2 * j + g] = rope(yt[base:base + 64]).astype(F32) * 0.125
                kn[2 * j + g] = rope(yt[base + 64:base + 128])
                vn[2 * j + g] = yt[base + 128:base + 192].astype(BF16)

    def insert(ref, l, s, h, new):
        mask = posb[...] == s.astype(BF16)
        page = ref[l, s, h].reshape(4, 16, 256)
        page = jnp.where(mask[None], new, page).reshape(64, 256)
        ref[l, s, h] = page
        return page.astype(F32)

    def heads(l, h0, h1):
        slot = lax.broadcasted_iota(jnp.int32, (32, 256), 0)
        keep = slot <= pos

        def one_head(h, carry):
            knew = kn[h].reshape(4, 16, 256)
            vnew = vn[h].reshape(4, 16, 256)

            def score(s, carry):
                page = insert(ko_ref, l, s, h, knew)
                sc[pl.ds(s, 1), :] = jnp.sum(page * qs[h], axis=0, keepdims=True)
                return carry

            lax.fori_loop(0, 32, score, 0, unroll=8)
            sm = jnp.where(keep, sc[...], -jnp.inf)
            ex = jnp.exp(sm - jnp.max(sm, axis=0, keepdims=True))
            probs = ex / jnp.sum(ex, axis=0, keepdims=True)
            pr[...] = probs.astype(BF16).astype(F32)

            def mix(s, acc):
                page = insert(vo_ref, l, s, h, vnew)
                return acc + page * pr[pl.ds(s, 1), :]

            ctx = lax.fori_loop(0, 32, mix, jnp.zeros((64, 256), F32), unroll=8)
            ctxt[h] = ctx.astype(BF16).astype(F32)
            return carry

        lax.fori_loop(h0, h1, one_head, 0)

    def attn_out(l):
        ctx = ctxt[...].reshape(512, 256).T.astype(BF16)
        w = wo[l].reshape(512, 512)
        accr[...] = jnp.dot(ctx, w, preferred_element_type=F32) + lnp[l, 4]

    def mlp_in(l):
        def chunk(n, carry):
            cols = pl.ds(pl.multiple_of(n * 256, 256), 256)
            w = wi[l, :, :, :, :, :, cols].reshape(512, 256)
            y = jnp.dot(h2s[...], w, preferred_element_type=F32) + bin_[l, n]
            act[:, cols] = gelu(y).astype(BF16)
            return carry

        lax.fori_loop(0, 8, chunk, 0)

    def mlp_down(l):
        for j in range(2):
            cols = slice(256 * j, 256 * (j + 1))
            w = wd[l, :, :, :, :, :, cols].reshape(2048, 256)
            m = jnp.dot(act[...], w, preferred_element_type=F32) + lnp[l, 5][:, cols]
            hcur[:, cols] = (hcur[:, cols].astype(F32) + accr[:, cols] + m).astype(BF16)

    qkv_stage(0)
    c(2)
    cache[0].wait()
    cache[1].wait()
    heads(0, 0, 4)
    d(1)
    heads(0, 4, 8)
    a(5)
    b(4)
    attn_out(0)
    e(1)
    c(3)
    mlp_in(0)
    d(2)
    e(2)
    b(5)
    mlp_down(0)
    d(3)
    c(4)
    e(3)
    qkv_stage(1)
    cache[2].wait()
    cache[3].wait()
    heads(1, 0, 4)
    c(5)
    d(4)
    heads(1, 4, 8)
    attn_out(1)
    e(4)
    mlp_in(1)
    d(5)
    e(5)
    mlp_down(1)
    out_ref[...] = (normalize(hcur[...].astype(F32)) * lnp[0, 6] + lnp[1, 6]).astype(BF16)
    for copy in sends.values():
        copy.wait_send()


def solution(mesh):
    row_spec = P('dp', None)
    vec_spec = P(None, 'dp')
    mat_spec = P(None, 'dp', None)
    cache_spec = P(None, 'dp', None, None, None)
    in_specs = (row_spec, P('dp'), cache_spec, cache_spec, vec_spec, vec_spec, vec_spec, vec_spec, mat_spec, vec_spec, mat_spec, vec_spec, mat_spec, vec_spec, mat_spec, vec_spec, P('dp'), P('dp'))
    out_specs = (row_spec, cache_spec, cache_spec)

    def device_step(x_embed, positions, k_cache, v_cache, ln1_gain, ln1_bias, ln2_gain, ln2_bias, w_qkv, b_qkv, w_out, b_out, w_in, b_in, w_down, b_down, lnf_gain, lnf_bias):
        pad = jnp.zeros((2, 32), BF16)
        lnf = jnp.stack([lnf_gain, lnf_bias])
        vec = jnp.concatenate([ln1_gain, ln1_bias, ln2_gain, ln2_bias, b_out, b_down, lnf, pad, b_qkv, pad, b_in], axis=1)
        vec = vec.reshape(8, 128)
        to_lanes = (0, 2, 3, 4, 1)
        kt = jnp.transpose(k_cache, to_lanes)
        vt = jnp.transpose(v_cache, to_lanes)
        vmem = pl.BlockSpec(memory_space=pltpu.VMEM)
        hbm = pl.BlockSpec(memory_space=pl.ANY)
        cache_shape = (2, 32, 8, 64, 256)
        out, ko, vo = pl.pallas_call(
            kernel,
            out_shape=(jax.ShapeDtypeStruct((256, 512), BF16),
                       pltpu.VMEM(cache_shape, BF16), pltpu.VMEM(cache_shape, BF16)),
            in_specs=[vmem, vmem, hbm, hbm, hbm, hbm, hbm, hbm, hbm],
            out_specs=(vmem, vmem, vmem),
            scratch_shapes=[
                pltpu.VMEM(GRID + (32, 1536), BF16),
                pltpu.VMEM(GRID + (32, 512), BF16),
                pltpu.VMEM(GRID + (32, 2048), BF16),
                pltpu.VMEM(GRID + (128, 512), BF16),
                pltpu.VMEM((1,) + GRID[1:] + (8, 128), BF16),
                pltpu.VMEM((2, 8, 1, 512), F32),
                pltpu.VMEM((2, 1, 1536), F32),
                pltpu.VMEM((2, 8, 1, 256), F32),
                pltpu.VMEM((8, 64, 256), F32),
                pltpu.VMEM((8, 64, 256), BF16),
                pltpu.VMEM((8, 64, 256), BF16),
                pltpu.VMEM((32, 256), F32),
                pltpu.VMEM((32, 256), F32),
                pltpu.VMEM((8, 64, 256), F32),
                pltpu.VMEM((256, 512), BF16),
                pltpu.VMEM((256, 512), BF16),
                pltpu.VMEM((256, 2048), BF16),
                pltpu.VMEM((256, 512), F32),
                pltpu.VMEM((16, 256), BF16),
                pltpu.SemaphoreType.DMA((9,)),
                pltpu.SemaphoreType.DMA((4,)),
                pltpu.SemaphoreType.DMA((N_ITEMS, 5)),
                pltpu.SemaphoreType.DMA((N_ITEMS, 5)),
            ],
            compiler_params=pltpu.CompilerParams(
                collective_id=0, has_side_effects=True, vmem_limit_bytes=26 * 2 ** 20),
        )(x_embed, positions.reshape(1, 256), vec, w_qkv, w_out, w_in, w_down, kt, vt)
        back = (0, 4, 1, 2, 3)
        return out, jnp.transpose(ko, back), jnp.transpose(vo, back)

    return jax.shard_map(device_step, mesh=mesh, in_specs=in_specs, out_specs=out_specs, check_vma=False)
```

profile of v0, /device:TPU:0, one launch (start us, length us, event | category | flops | bytes accessed | tf_op | source)
XLA Modules:
  0.0 71.5 jit_solution(4432588228951341061)
XLA Ops:
  0.6 0.7 pad_maximum_fusion
  1.3 0.9 %concatenate.3 = bf16[2,512]{1,0:T(2,128)(2,1)S(1)} concatenate(bf16[2,32]{1,0:T(2,128)(2,1)} %param.22, bf16[2,32]{1,0:T(2,128)(2,1)} %param.23, bf16[2,32]{1,0:T(2,128)(2,1)} %param.24, bf16[2,32]{1,0:T(2,128)(2,1)} %param.25, bf16[2,32]{1,0:T(2,128)(2,1)} %param.29, bf16[2,32]{1,0:T(2,128)(2,1)} %param.33, bf16[2,32]{1,0:T(2,128)(2,1)S(1)} %pad_maximum_fusion, ...), dimensions={1} | concatenate | bytes 4096 | tf_op jit(solution)/shard_map/concatenate | solution.py:341
  2.2 0.6 reshape.13.vec_in
  2.8 55.7 %shard_map.193 = (bf16[256,512]{1,0:T(8,128)(2,1)}, bf16[2,32,8,64,256]{4,3,2,1,0:T(8,128)(2,1)S(1)}, bf16[2,32,8,64,256]{4,3,2,1,0:T(8,128)(2,1)S(1)}) custom-call(bf16[256,512]{1,0:T(8,128)(2,1)} %x_ref.1, s32[1,256]{1,0:T(1,128)} %bitcast.11, bf16[8,128]{1,0:T(8,128)(2,1)} %reshape.13.vec_in, bf16[2,32,1536]{2,1,0:T(8,128)(2,1)} %wq_in.1, ...), custom_call_target="tpu_custom_call" | custom-call | tf_op jit(solution)/shard_map/pallas_call | solution.py:349
  58.5 6.2 %copy.24 = bf16[2,256,32,8,64]{1,4,3,2,0:T(8,128)(2,1)} copy(bf16[2,256,32,8,64]{1,4,3,2,0:T(8,128)(2,1)S(1)} %bitcast.8) | data formatting | bytes 33554432
  64.6 0.0 copy-start
  64.7 6.2 %copy.25 = bf16[2,256,32,8,64]{1,4,3,2,0:T(8,128)(2,1)} copy(bf16[2,256,32,8,64]{1,4,3,2,0:T(8,128)(2,1)S(1)} %bitcast.7) | data formatting | bytes 33554432
  70.8 0.0 copy-done
  70.8 0.7 copy.26
  (1 shorter events, 0.0 us)
Async XLA Ops:
  64.6 6.2 %copy-start = (bf16[256,512]{1,0:T(8,128)(2,1)S(1)}, bf16[256,512]{1,0:T(8,128)(2,1)}, u32[]{:S(2)}) copy-start(bf16[256,512]{1,0:T(8,128)(2,1)} %get-tuple-element.15) | copy-start | bytes 786436
where the time goes:
time: 71.7 us; the launch traced here: 71.5 us
  Pallas kernels  55.7 us (78%)
  local copies, waits for them, and re-layouts  14.5 us (20%)
    pallas_call x1, Pallas kernels, device_step(): pl.pallas_call(kernel, out_shape=(jax.ShapeDtypeStruct((256, 512), BF16),...  55.7 us
    unnamed x5, local copies, waits for them, and re-layouts  13 us

commit v1 on v0

v1 whole, which is shorter than its diff:
```python
import jax
import jax.numpy as jnp
from jax import lax
from jax.experimental import pallas as pl
from jax.experimental.pallas import tpu as pltpu
from jax.sharding import PartitionSpec as P

LN_EPS = 1e-5
ROPE_BASE = 10000.0
F32 = jnp.float32
BF16 = jnp.bfloat16
MESH = pl.DeviceIdType.MESH
GRID = (2,) * 5
LAYERS, SEQS, WIDTH, SLOTS, HEADS, HEAD, LANES, FF = 2, 256, 512, 32, 8, 64, 128, 2048
PAIR = 6 * HEAD
EARLY = 2
ALL = slice(None)
SCOPED = 22 * 2 ** 20

ERF_NUM = (-2.72614225801306e-10, 2.77068142495902e-08, -2.10102402082508e-06,
           -5.69250639462346e-05, -7.34990630326855e-04, -2.95459980854025e-03,
           -1.60960333262415e-02)
ERF_DEN = (-1.45660718464996e-05, -2.13374055278905e-04, -1.68282697438203e-03,
           -7.37332916720468e-03, -1.42647390514189e-02)


def horner(coefs, t):
    acc = jnp.full_like(t, coefs[0])
    for coef in coefs[1:]:
        acc = acc * t + coef
    return acc


def gelu(v):
    u = jnp.clip(v * (0.5 ** 0.5), -4.0, 4.0)
    t = u * u
    erf = u * horner(ERF_NUM, t) / horner(ERF_DEN, t)
    return 0.5 * v * (1.0 + erf)


def normalize(v):
    centered = v - jnp.mean(v, axis=-1, keepdims=True)
    var = jnp.mean(centered * centered, axis=-1, keepdims=True)
    return centered * lax.rsqrt(var + LN_EPS)


def dot(a, b):
    return jnp.dot(a, b, preferred_element_type=F32)


def iota(shape, axis):
    return lax.broadcasted_iota(jnp.int32, shape, axis)


def pieces(l):
    rows = (l, 0, SLOTS)
    third = 5 * LANES
    qo = [(0, *rows, 0, third, 0), (0, *rows, third, third, 1),
          (0, *rows, 2 * third, 2 * LANES, 2), (1, *rows, 0, WIDTH, 2)]
    up = [(2, *rows, 0, third, 0), (2, *rows, third, third, 1), (2, *rows, 2 * third, 6 * LANES, 2)]
    down = [(3, l, 0, 48, 0, WIDTH, 0), (3, l, 48, 48, 0, WIDTH, 1), (3, l, 96, SLOTS, 0, WIDTH, 2)]
    return [qo, up, down]


PIECES = pieces(0) + pieces(1) + [[(4, 0, 0, HEADS, 0, LANES, 0)]]
VEC = len(PIECES) - 1
N_VEC = 10
ITEMS = [item for piece in PIECES for item in piece]
FIRST = [sum(len(piece) for piece in PIECES[:p]) for p in range(len(PIECES) + 1)]


def attend(h, pos, posb, qs, kn, vn, k_in, v_in, k_out, v_out, sc, pr, ctxt):
    tiles = (HEAD // 16, 16, SEQS)
    knew = kn[h].reshape(tiles)
    vnew = vn[h].reshape(tiles)

    def insert(src, dst, s, new):
        mask = posb[...] == s.astype(BF16)
        page = jnp.where(mask[None], new, src(s).reshape(tiles)).reshape(HEAD, SEQS)
        dst(s, page)
        return page.astype(F32)

    def score(s, carry):
        page = insert(k_in, k_out, s, knew)
        sc[pl.ds(s, 1), :] = jnp.sum(page * qs[h], axis=0, keepdims=True)
        return carry

    lax.fori_loop(0, SLOTS, score, 0, unroll=8)
    sm = jnp.where(iota((SLOTS, SEQS), 0) <= pos, sc[...], -jnp.inf)
    ex = jnp.exp(sm - jnp.max(sm, axis=0, keepdims=True))
    probs = ex / jnp.sum(ex, axis=0, keepdims=True)
    pr[...] = probs.astype(BF16).astype(F32)

    def mix(s, acc):
        page = insert(v_in, v_out, s, vnew)
        return acc + page * pr[pl.ds(s, 1), :]

    ctx = lax.fori_loop(0, SLOTS, mix, jnp.zeros((HEAD, SEQS), F32), unroll=8)
    ctxt[h] = ctx.astype(BF16).astype(F32)


def attn_out(ctxt, w, bias):
    ctx = ctxt[...].reshape(WIDTH, SEQS).T.astype(BF16)
    return dot(ctx, w.reshape(WIDTH, WIDTH)) + bias


def gather_kernel(x_ref, pos_ref, *refs):
    gather_body(x_ref, pos_ref, refs[:N_VEC], *refs[N_VEC:])


def gather_body(x_ref, pos_ref, vec_in, wq_in, wo_in, wi_in, wd_in, kc_in, vc_in,
                  ko0, vo0, ko1, vo1, wo1, wd1, qs, kn, vn, ctxt, hcur, act, lnp,
                  wq, wo0, wi, wd0, vecs, bqkv, bin_, sc, pr, h2s, accr, posb,
                  local_sem, cache_sem, send_sem, recv_sem):
    me = lax.axis_index('dp')
    core = me % 2
    px = (me // 2) % 2
    py = (me // 4) % 2
    pz = me // 8
    place = (px, py, pz)
    peer_core = me + 1 - 2 * core
    peers = (me + 2 - 4 * px, me + 4 - 8 * py, me + 8 - 16 * pz)
    shards = (wq_in, wo_in, wi_in, wd_in)

    def whole(m, l):
        if m == 4:
            return vecs
        return ((wq.at[0], wo0, wi.at[0], wd0), (wq.at[1], wo1, wi.at[1], wd1))[l][m]

    local = {}
    for l, m in [(l, m) for l in range(LAYERS) for m in range(4)]:
        local[(m, l)] = pltpu.make_async_copy(
            shards[m].at[l], whole(m, l).at[pz, py, px, core], local_sem.at[len(local)])
        local[(m, l)].start()

    barrier = pltpu.get_barrier_semaphore()
    for peer in peers + (peer_core,):
        pl.semaphore_signal(barrier, inc=1, device_id=(peer,), device_id_type=MESH)
    g1, b1, g2, b2, bo, bd, bq, bi, gf, bf = (ref[...].astype(F32) for ref in vec_in)
    pad = jnp.zeros((LAYERS, 32), F32)
    groups = ([g1, b1, g2, b2], [bo, bd, jnp.concatenate([gf, bf], axis=0), pad], [bq, pad])
    rows = [jnp.concatenate(group, axis=1) for group in groups] + [bi]
    vecs[pz, py, px, core] = jnp.concatenate(rows, axis=0).astype(BF16)
    pl.semaphore_wait(barrier, len(peers) + 1)

    sends = {}

    def send(i, stage):
        m, l, r0, rn, c0, cn, o = ITEMS[i]
        axes = [(o + s) % 3 for s in range(3)]
        at = [place[2], place[1], place[0]]
        for ax in axes[:min(stage, 2)]:
            at[2 - ax] = ALL
        if stage == 4:
            at[2 - axes[2]] = 1 - place[axes[2]]
        ref = whole(m, l).at[(*at, core, pl.ds(r0, rn), pl.ds(c0, cn))]
        peer = peers[axes[stage]] if stage < 3 else peer_core
        copy = pltpu.make_async_remote_copy(
            src_ref=ref, dst_ref=ref, send_sem=send_sem.at[i, stage],
            recv_sem=recv_sem.at[i, stage], device_id=(peer,), device_id_type=MESH)
        copy.start()
        sends[(i, stage)] = copy

    def ids(p):
        return range(FIRST[p], FIRST[p + 1])

    waited = set()

    def a(p):
        for i in ids(p):
            key = ITEMS[i][:2]
            if key in local and key not in waited:
                waited.add(key)
                local[key].wait()
        for i in ids(p):
            send(i, 0)

    def b(p):
        for i in ids(p):
            sends[(i, 0)].wait_recv()
            send(i, 1)

    def c(p):
        for i in ids(p):
            sends[(i, 1)].wait_recv()
            send(i, 2)
            send(i, 3)

    def d(p):
        for i in ids(p):
            sends[(i, 2)].wait_recv()
            send(i, 4)

    def e(p):
        for i in ids(p):
            sends[(i, 3)].wait_recv()
            sends[(i, 4)].wait_recv()

    a(0)
    a(VEC)
    a(1)
    a(2)
    cache = []
    ko, vo = (ko0, ko1), (vo0, vo1)
    for l in range(LAYERS):
        for src, dst in ((kc_in, ko), (vc_in, vo)):
            cache.append(pltpu.make_async_copy(src.at[l], dst[l], cache_sem.at[len(cache)]))
            cache[-1].start()

    pos = pos_ref[...]
    posf = pos.astype(F32)
    posb[...] = jnp.broadcast_to(posf, posb.shape).astype(BF16)
    half = (8, SEQS)
    inv_freq = jnp.full(half, 1.0, F32)
    for i in range(1, 8):
        inv_freq = jnp.where(iota(half, 0) == i, F32(ROPE_BASE ** (-i / 8.0)), inv_freq)
    angle = jnp.broadcast_to(posf, half) * inv_freq
    cos_t = jnp.cos(angle)
    sin_t = jnp.sin(angle)
    hcur[...] = x_ref[...]

    b(VEC)
    b(0)
    b(1)
    c(VEC)
    c(0)
    a(3)
    b(2)
    d(VEC)
    e(VEC)

    vall = vecs[...].reshape(16, 8, LANES).astype(F32)
    wide_shape = (16, WIDTH)
    spread = jnp.where(iota((LANES, WIDTH), 0) % 32 == iota((LANES, WIDTH), 1) % 32, 1.0, 0.0).astype(BF16)
    own = iota(wide_shape, 1) // 32 == iota(wide_shape, 0)
    quarter = iota((16, LANES), 1) // 32
    qkv_shape = (LANES, 3 * WIDTH)
    spread_q = jnp.where(iota(qkv_shape, 0) == iota(qkv_shape, 1) % 96, 1.0, 0.0).astype(BF16)
    own_q = iota((16, 3 * WIDTH), 1) // 96 == iota((16, 3 * WIDTH), 0)

    def collapse(mask, part, table):
        return jnp.sum(jnp.where(mask, dot(part.astype(BF16), table), 0.0), axis=0, keepdims=True)

    for l in range(LAYERS):
        for k in range(7):
            part = jnp.where(quarter == k % 4, vall[:, 2 * (k // 4) + l, :], 0.0)
            lnp[l, k] = collapse(own, part, spread)
        bqkv[l] = collapse(own_q, vall[:, 4 + l, :], spread_q)
        share = vall[:, 6 + l, :]
        for n in range(8):
            bin_[l, n] = jnp.concatenate([share[2 * n:2 * n + 1], share[2 * n + 1:2 * n + 2]], axis=1)

    def rope(t):
        r1, r2 = t[:8], t[8:16]
        rot = jnp.concatenate([r1 * cos_t - r2 * sin_t, r2 * cos_t + r1 * sin_t, t[16:]], axis=0)
        return rot.astype(BF16)

    def qkv_stage(l):
        normed = normalize(hcur[...].astype(F32))
        h1 = (normed * lnp[l, 0] + lnp[l, 1]).astype(BF16)
        h2s[...] = (normed * lnp[l, 2] + lnp[l, 3]).astype(BF16)
        for j in range(HEADS // 2):
            cols = slice(PAIR * j, PAIR * (j + 1))
            y = dot(h1, whole(0, l)[:, :, :, :, :, cols].reshape(WIDTH, PAIR)) + bqkv[l][:, cols]
            yt = y.astype(BF16).astype(F32).T
            for g in range(2):
                q, k, v = (yt[HEAD * (3 * g + i):HEAD * (3 * g + i + 1)] for i in range(3))
                qs[2 * j + g] = rope(q).astype(F32) * (HEAD ** -0.5)
                kn[2 * j + g] = rope(k)
                vn[2 * j + g] = v.astype(BF16)

    def heads(l, h0, h1):
        def one_head(h, carry):
            def put(ref):
                def store(s, page):
                    ref[s, h] = page
                return store
            attend(h, pos, posb, qs, kn, vn, lambda s: ko[l][s, h], lambda s: vo[l][s, h],
                   put(ko[l]), put(vo[l]), sc, pr, ctxt)
            return carry

        lax.fori_loop(h0, h1, one_head, 0)

    def mlp_in(l, n0, n1):
        def chunk(n, carry):
            cols = pl.ds(pl.multiple_of(n * SEQS, SEQS), SEQS)
            w = whole(2, l)[:, :, :, :, :, cols].reshape(WIDTH, SEQS)
            y = dot(h2s[...], w) + bin_[l, n]
            act[:, cols] = gelu(y).astype(BF16)
            return carry

        lax.fori_loop(n0, n1, chunk, 0)

    c(1)
    d(0)
    a(4)
    b(3)
    e(0)
    c(2)
    qkv_stage(0)
    cache[0].wait()
    cache[1].wait()
    heads(0, 0, 4)
    a(5)
    b(4)
    d(1)
    heads(0, 4, 6)
    c(3)
    heads(0, 6, HEADS)
    accr[...] = attn_out(ctxt, wo0[...], lnp[0, 4])
    e(1)
    b(5)
    mlp_in(0, 0, 4)
    d(2)
    mlp_in(0, 4, 8)
    c(4)
    e(2)
    for j in range(2):
        cols = slice(SEQS * j, SEQS * (j + 1))
        m = dot(act[...], wd0[:, :, :, :, :, cols].reshape(FF, SEQS)) + lnp[0, 5][:, cols]
        hcur[:, cols] = (hcur[:, cols].astype(F32) + accr[:, cols] + m).astype(BF16)
    d(3)
    c(5)
    e(3)
    qkv_stage(1)
    cache[2].wait()
    cache[3].wait()
    heads(1, 0, EARLY)
    d(4)
    e(4)
    mlp_in(1, 0, 4)
    d(5)
    mlp_in(1, 4, 8)
    e(5)
    for copy in sends.values():
        copy.wait_send()


def finish_kernel(ko0, vo0, ko1, vo1, wo1, wd1, qs, kn, vn, ctxt, hcur, act, lnp, pos_ref,
                  out_ref, k_hbm, v_hbm, kst, vst, ctxs, sc, pr, posb, sems):
    last = LAYERS - 1
    copies = []

    def write(src, dst):
        copies.append(pltpu.make_async_copy(src, dst, sems.at[len(copies)]))
        copies[-1].start()

    for src, dst in ((ko0, k_hbm), (vo0, v_hbm)):
        for g in range(2):
            part = pl.ds(g * (SLOTS // 2), SLOTS // 2)
            write(src.at[part], dst.at[0, part])
    for src, dst in ((ko1, k_hbm), (vo1, v_hbm)):
        write(src.at[:, pl.ds(0, EARLY)], dst.at[last, :, pl.ds(0, EARLY)])
    pos = pos_ref[...]
    posb[...] = jnp.broadcast_to(pos.astype(F32), posb.shape).astype(BF16)
    ctxs[...] = ctxt[...]

    def put(ref, i):
        def store(s, page):
            ref[i, s] = page
        return store

    for i in range(HEADS - EARLY):
        h = EARLY + i
        attend(h, pos, posb, qs, kn, vn, lambda s: ko1[s, h], lambda s: vo1[s, h],
               put(kst, i), put(vst, i), sc, pr, ctxs)
        write(kst.at[i], k_hbm.at[last, :, h])
        write(vst.at[i], v_hbm.at[last, :, h])
    x = attn_out(ctxs, wo1[...], lnp[last, 4])
    m = dot(act[...], wd1[...].reshape(FF, WIDTH)) + lnp[last, 5]
    x = (hcur[...].astype(F32) + x + m).astype(BF16).astype(F32)
    out_ref[...] = (normalize(x) * lnp[0, 6] + lnp[1, 6]).astype(BF16)
    for copy in copies:
        copy.wait()


def solution(mesh):
    row_spec = P('dp', None)
    vec_spec = P(None, 'dp')
    mat_spec = P(None, 'dp', None)
    cache_spec = P(None, 'dp', None, None, None)
    in_specs = (row_spec, P('dp'), cache_spec, cache_spec, vec_spec, vec_spec, vec_spec, vec_spec, mat_spec, vec_spec, mat_spec, vec_spec, mat_spec, vec_spec, mat_spec, vec_spec, P('dp'), P('dp'))
    out_specs = (row_spec, cache_spec, cache_spec)

    def device_step(x_embed, positions, k_cache, v_cache, ln1_gain, ln1_bias, ln2_gain, ln2_bias, w_qkv, b_qkv, w_out, b_out, w_in, b_in, w_down, b_down, lnf_gain, lnf_bias):
        vectors = (ln1_gain, ln1_bias, ln2_gain, ln2_bias, b_out, b_down, b_qkv, b_in,
                   lnf_gain.reshape(1, 32), lnf_bias.reshape(1, 32))
        to_lanes = (0, 2, 3, 4, 1)
        kt = jnp.transpose(k_cache, to_lanes)
        vt = jnp.transpose(v_cache, to_lanes)
        pos = positions.reshape(1, SEQS)
        vmem = pl.BlockSpec(memory_space=pltpu.VMEM)
        hbm = pl.BlockSpec(memory_space=pl.ANY)
        cache_shape = (LAYERS, SLOTS, HEADS, HEAD, SEQS)
        head_shape = (HEADS, HEAD, SEQS)
        out_w = GRID[1:] + (SLOTS, WIDTH)
        down_w = GRID[1:] + (LANES, WIDTH)
        carried = [pltpu.VMEM(shape, dtype) for shape, dtype in (
            *[(cache_shape[1:], BF16)] * 4, (out_w, BF16), (down_w, BF16),
            (head_shape, F32), (head_shape, BF16), (head_shape, BF16), (head_shape, F32),
            ((SEQS, WIDTH), BF16), ((SEQS, FF), BF16), ((LAYERS, 8, 1, WIDTH), F32))]
        state = pl.pallas_call(
            gather_kernel,
            out_shape=carried,
            in_specs=[vmem] * (2 + N_VEC) + [hbm] * 6,
            out_specs=[vmem] * len(carried),
            scratch_shapes=[
                pltpu.VMEM(GRID + (SLOTS, 3 * WIDTH), BF16),
                pltpu.VMEM(out_w, BF16),
                pltpu.VMEM(GRID + (SLOTS, FF), BF16),
                pltpu.VMEM(down_w, BF16),
                pltpu.VMEM(GRID[1:] + (8, LANES), BF16),
                pltpu.VMEM((LAYERS, 1, 3 * WIDTH), F32),
                pltpu.VMEM((LAYERS, 8, 1, SEQS), F32),
                pltpu.VMEM((SLOTS, SEQS), F32),
                pltpu.VMEM((SLOTS, SEQS), F32),
                pltpu.VMEM((SEQS, WIDTH), BF16),
                pltpu.VMEM((SEQS, WIDTH), F32),
                pltpu.VMEM((16, SEQS), BF16),
                pltpu.SemaphoreType.DMA((8,)),
                pltpu.SemaphoreType.DMA((4,)),
                pltpu.SemaphoreType.DMA((len(ITEMS), 5)),
                pltpu.SemaphoreType.DMA((len(ITEMS), 5)),
            ],
            compiler_params=pltpu.CompilerParams(
                collective_id=0, has_side_effects=True, vmem_limit_bytes=SCOPED),
        )(x_embed, pos, *vectors, w_qkv, w_out, w_in, w_down, kt, vt)
        state = [pltpu.with_memory_space_constraint(array, pltpu.VMEM) for array in state]
        stage = pltpu.VMEM((HEADS - EARLY, SLOTS, HEAD, SEQS), BF16)
        out, ko, vo = pl.pallas_call(
            finish_kernel,
            out_shape=(jax.ShapeDtypeStruct((SEQS, WIDTH), BF16),
                       pltpu.HBM(cache_shape, BF16), pltpu.HBM(cache_shape, BF16)),
            in_specs=[vmem] * (len(carried) + 1),
            out_specs=(vmem, pl.BlockSpec(memory_space=pltpu.HBM), pl.BlockSpec(memory_space=pltpu.HBM)),
            scratch_shapes=[
                stage, stage,
                pltpu.VMEM(head_shape, F32),
                pltpu.VMEM((SLOTS, SEQS), F32),
                pltpu.VMEM((SLOTS, SEQS), F32),
                pltpu.VMEM((16, SEQS), BF16),
                pltpu.SemaphoreType.DMA((6 + 2 * (HEADS - EARLY),)),
            ],
            compiler_params=pltpu.CompilerParams(vmem_limit_bytes=SCOPED),
        )(*state, pos)
        back = (0, 4, 1, 2, 3)
        return out, jnp.transpose(ko, back), jnp.transpose(vo, back)

    return jax.shard_map(device_step, mesh=mesh, in_specs=in_specs, out_specs=out_specs, check_vma=False)
```

time: 71.7 us -> 64.7 us (0.902)
  local copies, waits for them, and re-layouts: 14.5 us -> 0 us
  Pallas kernels: 55.7 us -> 63.9 us
    unnamed x5 -> x0, local copies, waits for them, and re-layouts: 13 us -> none
    pallas_call x1 -> x2, Pallas kernels: 55.7 us -> 63.9 us  [the longest x1 51.5 us: device_step(): pl.pallas_call(gather_kernel, out_shape=carried, in_specs=[vmem] * (2 + N...]
    concatenate x1 -> x0, local copies, waits for them, and re-layouts: 0.87 us -> none  [device_step(): jnp.concatenate([ln1_gain, ln1_bias, ln2_gain, ln2_bias, b_out, b_down, l...]
where the time goes in v1:
time: 64.7 us; the launch traced here: 64.5 us
  Pallas kernels  63.9 us (99%)
  between operations  0.65 us (1%)
    pallas_call x1, Pallas kernels, device_step(): pl.pallas_call(gather_kernel, out_shape=carried, in_specs=[vmem] * (2 + N...  51.5 us
    pallas_call x1, Pallas kernels, device_step(): pl.pallas_call(finish_kernel, out_shape=(jax.ShapeDtypeStruct((SEQS, WIDT...  12.4 us

profile of v1, /device:TPU:0, one launch (start us, length us, event | category | flops | bytes accessed | tf_op | source)
XLA Modules:
  0.0 64.5 jit_solution(10669176200476945586)
XLA Ops:
  0.6 51.5 %shard_map.193 = (bf16[32,8,64,256]{3,2,1,0:T(8,128)(2,1)S(1)}, bf16[32,8,64,256]{3,2,1,0:T(8,128)(2,1)S(1)}, bf16[32,8,64,256]{3,2,1,0:T(8,128)(2,1)S(1)}, bf16...) custom-call(bf16[256,512]{1,0:T(8,128)(2,1)} %x_ref.1, ...), custom_call_target="tpu_custom_call" | custom-call | tf_op jit(solution)/shard_map/pallas_call | solution.py:402
  52.1 12.4 %shard_map.194 = (bf16[256,512]{1,0:T(8,128)(2,1)}, bf16[2,32,8,64,256]{4,3,2,1,0:T(8,128)(2,1)}, bf16[2,32,8,64,256]{4,3,2,1,0:T(8,128)(2,1)}) custom-call(bf16[32,8,64,256]{3,2,1,0:T(8,128)(2,1)S(1)} %get-tuple-element.19.ko0, bf16[32,8,64,256]{3,2,1,0:T(8,128)(2,1)S(1)} %get-tuple-element.20.vo0, bf16[32,8,64,256]{3,2,1,0:T(8,128)(2,1)S(1)} %get-tuple-element.21.ko1, ...), custom_call_target="tpu_custom_call" | custom-call | tf_op jit(solution)/shard_map/pallas_call | solution.py:430

commit v2 on v1

--- a/solution.py
+++ b/solution.py
@@ -15,7 +15,7 @@
 PAIR = 6 * HEAD
 EARLY = 2
 ALL = slice(None)
-SCOPED = 22 * 2 ** 20
+SCOPED = 20 * 2 ** 20
 
 ERF_NUM = (-2.72614225801306e-10, 2.77068142495902e-08, -2.10102402082508e-06,
            -5.69250639462346e-05, -7.34990630326855e-04, -2.95459980854025e-03,
@@ -104,14 +104,21 @@
     return dot(ctx, w.reshape(WIDTH, WIDTH)) + bias
 
 
-def gather_kernel(x_ref, pos_ref, *refs):
-    gather_body(x_ref, pos_ref, refs[:N_VEC], *refs[N_VEC:])
-
-
-def gather_body(x_ref, pos_ref, vec_in, wq_in, wo_in, wi_in, wd_in, kc_in, vc_in,
-                  ko0, vo0, ko1, vo1, wo1, wd1, qs, kn, vn, ctxt, hcur, act, lnp,
-                  wq, wo0, wi, wd0, vecs, bqkv, bin_, sc, pr, h2s, accr, posb,
-                  local_sem, cache_sem, send_sem, recv_sem):
+def mlp_in(h, w_ref, bias_ref, l, act, n0, n1):
+    for n in range(n0, n1):
+        cols = slice(n * SEQS, (n + 1) * SEQS)
+        w = w_ref[:, :, :, :, :, cols].reshape(WIDTH, SEQS)
+        act[:, cols] = gelu(dot(h[...], w) + bias_ref[l, n]).astype(BF16)
+
+
+def gather_kernel(x_in, pos_in, *refs):
+    gather_body(x_in, pos_in, refs[:N_VEC], *refs[N_VEC:-N_VEC], refs[-N_VEC:])
+
+
+def gather_body(x_in, pos_in, vec_in, wq_in, wo_in, wi_in, wd_in, kc_in, vc_in,
+                  ko0, vo0, ko1, vo1, wo1, wi1, wd1, qs, kn, vn, ctxt, hcur, h2s, lnp, bin_, pos_ref,
+                  wq, wo0, wi0, wd0, vecs, bqkv, sc, pr, act, accr, posb,
+                  local_sem, cache_sem, small_sem, send_sem, recv_sem, vec_ref):
     me = lax.axis_index('dp')
     core = me % 2
     px = (me // 2) % 2
@@ -125,22 +132,24 @@
     def whole(m, l):
         if m == 4:
             return vecs
-        return ((wq.at[0], wo0, wi.at[0], wd0), (wq.at[1], wo1, wi.at[1], wd1))[l][m]
+        return ((wq.at[0], wo0, wi0, wd0), (wq.at[1], wo1, wi1, wd1))[l][m]
 
     local = {}
     for l, m in [(l, m) for l in range(LAYERS) for m in range(4)]:
         local[(m, l)] = pltpu.make_async_copy(
             shards[m].at[l], whole(m, l).at[pz, py, px, core], local_sem.at[len(local)])
-        local[(m, l)].start()
-
+    for m in range(2):
+        local[(m, 0)].start()
     barrier = pltpu.get_barrier_semaphore()
     for peer in peers + (peer_core,):
         pl.semaphore_signal(barrier, inc=1, device_id=(peer,), device_id_type=MESH)
-    g1, b1, g2, b2, bo, bd, bq, bi, gf, bf = (ref[...].astype(F32) for ref in vec_in)
-    pad = jnp.zeros((LAYERS, 32), F32)
-    groups = ([g1, b1, g2, b2], [bo, bd, jnp.concatenate([gf, bf], axis=0), pad], [bq, pad])
-    rows = [jnp.concatenate(group, axis=1) for group in groups] + [bi]
-    vecs[pz, py, px, core] = jnp.concatenate(rows, axis=0).astype(BF16)
+    small = []
+    for src, dst in zip((*vec_in, pos_in, x_in), (*vec_ref, pos_ref, hcur)):
+        small.append(pltpu.make_async_copy(src, dst, small_sem.at[len(small)]))
+        small[-1].start()
+    for key, copy in local.items():
+        if key not in ((0, 0), (1, 0)):
+            copy.start()
     pl.semaphore_wait(barrier, len(peers) + 1)
 
     sends = {}
@@ -197,6 +206,13 @@
             sends[(i, 4)].wait_recv()
 
     a(0)
+    for copy in small[:N_VEC]:
+        copy.wait()
+    g1, b1, g2, b2, bo, bd, bq, bi, gf, bf = (ref[...].astype(F32) for ref in vec_ref)
+    pad = jnp.zeros((LAYERS, 32), F32)
+    groups = ([g1, b1, g2, b2], [bo, bd, jnp.concatenate([gf, bf], axis=0), pad], [bq, pad])
+    rows = [jnp.concatenate(group, axis=1) for group in groups] + [bi]
+    vecs[pz, py, px, core] = jnp.concatenate(rows, axis=0).astype(BF16)
     a(VEC)
     a(1)
     a(2)
@@ -207,6 +223,8 @@
             cache.append(pltpu.make_async_copy(src.at[l], dst[l], cache_sem.at[len(cache)]))
             cache[-1].start()
 
+    for copy in small[N_VEC:]:
+        copy.wait()
     pos = pos_ref[...]
     posf = pos.astype(F32)
     posb[...] = jnp.broadcast_to(posf, posb.shape).astype(BF16)
@@ -217,7 +235,6 @@
     angle = jnp.broadcast_to(posf, half) * inv_freq
     cos_t = jnp.cos(angle)
     sin_t = jnp.sin(angle)
-    hcur[...] = x_ref[...]
 
     b(VEC)
     b(0)
@@ -280,16 +297,6 @@
             return carry
 
         lax.fori_loop(h0, h1, one_head, 0)
-
-    def mlp_in(l, n0, n1):
-        def chunk(n, carry):
-            cols = pl.ds(pl.multiple_of(n * SEQS, SEQS), SEQS)
-            w = whole(2, l)[:, :, :, :, :, cols].reshape(WIDTH, SEQS)
-            y = dot(h2s[...], w) + bin_[l, n]
-            act[:, cols] = gelu(y).astype(BF16)
-            return carry
-
-        lax.fori_loop(n0, n1, chunk, 0)
 
     c(1)
     d(0)
@@ -310,9 +317,9 @@
     accr[...] = attn_out(ctxt, wo0[...], lnp[0, 4])
     e(1)
     b(5)
-    mlp_in(0, 0, 4)
+    mlp_in(h2s, wi0, bin_, 0, act, 0, 4)
     d(2)
-    mlp_in(0, 4, 8)
+    mlp_in(h2s, wi0, bin_, 0, act, 4, 8)
     c(4)
     e(2)
     for j in range(2):
@@ -328,16 +335,14 @@
     heads(1, 0, EARLY)
     d(4)
     e(4)
-    mlp_in(1, 0, 4)
     d(5)
-    mlp_in(1, 4, 8)
     e(5)
     for copy in sends.values():
         copy.wait_send()
 
 
-def finish_kernel(ko0, vo0, ko1, vo1, wo1, wd1, qs, kn, vn, ctxt, hcur, act, lnp, pos_ref,
-                  out_ref, k_hbm, v_hbm, kst, vst, ctxs, sc, pr, posb, sems):
+def finish_kernel(ko0, vo0, ko1, vo1, wo1, wi1, wd1, qs, kn, vn, ctxt, hcur, h2s, lnp, bin_, pos_ref,
+                  out_hbm, k_hbm, v_hbm, kst, vst, ctxs, sc, pr, posb, act, outs, sems):
     last = LAYERS - 1
     copies = []
 
@@ -366,10 +371,12 @@
                put(kst, i), put(vst, i), sc, pr, ctxs)
         write(kst.at[i], k_hbm.at[last, :, h])
         write(vst.at[i], v_hbm.at[last, :, h])
+    mlp_in(h2s, wi1, bin_, last, act, 0, 8)
     x = attn_out(ctxs, wo1[...], lnp[last, 4])
     m = dot(act[...], wd1[...].reshape(FF, WIDTH)) + lnp[last, 5]
     x = (hcur[...].astype(F32) + x + m).astype(BF16).astype(F32)
-    out_ref[...] = (normalize(x) * lnp[0, 6] + lnp[1, 6]).astype(BF16)
+    outs[...] = (normalize(x) * lnp[0, 6] + lnp[1, 6]).astype(BF16)
+    write(outs, out_hbm)
     for copy in copies:
         copy.wait()
 
@@ -394,33 +401,36 @@
         cache_shape = (LAYERS, SLOTS, HEADS, HEAD, SEQS)
         head_shape = (HEADS, HEAD, SEQS)
         out_w = GRID[1:] + (SLOTS, WIDTH)
+        in_w = GRID[1:] + (SLOTS, FF)
         down_w = GRID[1:] + (LANES, WIDTH)
         carried = [pltpu.VMEM(shape, dtype) for shape, dtype in (
-            *[(cache_shape[1:], BF16)] * 4, (out_w, BF16), (down_w, BF16),
+            *[(cache_shape[1:], BF16)] * 4, (out_w, BF16), (in_w, BF16), (down_w, BF16),
             (head_shape, F32), (head_shape, BF16), (head_shape, BF16), (head_shape, F32),
-            ((SEQS, WIDTH), BF16), ((SEQS, FF), BF16), ((LAYERS, 8, 1, WIDTH), F32))]
+            ((SEQS, WIDTH), BF16), ((SEQS, WIDTH), BF16), ((LAYERS, 8, 1, WIDTH), F32),
+            ((LAYERS, 8, 1, SEQS), F32), ((1, SEQS), jnp.int32))]
         state = pl.pallas_call(
             gather_kernel,
             out_shape=carried,
-            in_specs=[vmem] * (2 + N_VEC) + [hbm] * 6,
+            in_specs=[hbm] * (8 + N_VEC),
             out_specs=[vmem] * len(carried),
             scratch_shapes=[
                 pltpu.VMEM(GRID + (SLOTS, 3 * WIDTH), BF16),
                 pltpu.VMEM(out_w, BF16),
-                pltpu.VMEM(GRID + (SLOTS, FF), BF16),
+                pltpu.VMEM(in_w, BF16),
                 pltpu.VMEM(down_w, BF16),
                 pltpu.VMEM(GRID[1:] + (8, LANES), BF16),
                 pltpu.VMEM((LAYERS, 1, 3 * WIDTH), F32),
-                pltpu.VMEM((LAYERS, 8, 1, SEQS), F32),
                 pltpu.VMEM((SLOTS, SEQS), F32),
                 pltpu.VMEM((SLOTS, SEQS), F32),
-                pltpu.VMEM((SEQS, WIDTH), BF16),
+                pltpu.VMEM((SEQS, FF), BF16),
                 pltpu.VMEM((SEQS, WIDTH), F32),
                 pltpu.VMEM((16, SEQS), BF16),
                 pltpu.SemaphoreType.DMA((8,)),
                 pltpu.SemaphoreType.DMA((4,)),
+                pltpu.SemaphoreType.DMA((2 + N_VEC,)),
                 pltpu.SemaphoreType.DMA((len(ITEMS), 5)),
                 pltpu.SemaphoreType.DMA((len(ITEMS), 5)),
+                *[pltpu.VMEM(array.shape, BF16) for array in vectors],
             ],
             compiler_params=pltpu.CompilerParams(
                 collective_id=0, has_side_effects=True, vmem_limit_bytes=SCOPED),
@@ -429,20 +439,22 @@
         stage = pltpu.VMEM((HEADS - EARLY, SLOTS, HEAD, SEQS), BF16)
         out, ko, vo = pl.pallas_call(
             finish_kernel,
-            out_shape=(jax.ShapeDtypeStruct((SEQS, WIDTH), BF16),
+            out_shape=(pltpu.HBM((SEQS, WIDTH), BF16),
                        pltpu.HBM(cache_shape, BF16), pltpu.HBM(cache_shape, BF16)),
-            in_specs=[vmem] * (len(carried) + 1),
-            out_specs=(vmem, pl.BlockSpec(memory_space=pltpu.HBM), pl.BlockSpec(memory_space=pltpu.HBM)),
+            in_specs=[vmem] * len(carried),
+            out_specs=[pl.BlockSpec(memory_space=pltpu.HBM)] * 3,
             scratch_shapes=[
                 stage, stage,
                 pltpu.VMEM(head_shape, F32),
                 pltpu.VMEM((SLOTS, SEQS), F32),
                 pltpu.VMEM((SLOTS, SEQS), F32),
                 pltpu.VMEM((16, SEQS), BF16),
-                pltpu.SemaphoreType.DMA((6 + 2 * (HEADS - EARLY),)),
+                pltpu.VMEM((SEQS, FF), BF16),
+                pltpu.VMEM((SEQS, WIDTH), BF16),
+                pltpu.SemaphoreType.DMA((7 + 2 * (HEADS - EARLY),)),
             ],
             compiler_params=pltpu.CompilerParams(vmem_limit_bytes=SCOPED),
-        )(*state, pos)
+        )(*state)
         back = (0, 4, 1, 2, 3)
         return out, jnp.transpose(ko, back), jnp.transpose(vo, back)
 

time: 64.7 us -> 60.6 us (0.937)
  Pallas kernels: 63.9 us -> 59.8 us
    pallas_call x2, Pallas kernels: 63.9 us -> 59.8 us  [the longest x1 48.8 us: device_step(): pl.pallas_call(gather_kernel, out_shape=carried, in_specs=[hbm] * (8 + N_...]
where the time goes in v2:
time: 60.6 us; the launch traced here: 60.5 us
  Pallas kernels  59.8 us (99%)
  between operations  0.65 us (1%)
    pallas_call x1, Pallas kernels, device_step(): pl.pallas_call(gather_kernel, out_shape=carried, in_specs=[hbm] * (8 + N_...  48.8 us
    pallas_call x1, Pallas kernels, device_step(): pl.pallas_call(finish_kernel, out_shape=(pltpu.HBM((SEQS, WIDTH), BF16),...  11.1 us

profile of v2, /device:TPU:0, one launch (start us, length us, event | category | flops | bytes accessed | tf_op | source)
XLA Modules:
  0.0 60.5 jit_solution(10561014660344767827)
XLA Ops:
  0.6 48.8 %shard_map.193 = (bf16[32,8,64,256]{3,2,1,0:T(8,128)(2,1)S(1)}, bf16[32,8,64,256]{3,2,1,0:T(8,128)(2,1)S(1)}, bf16[32,8,64,256]{3,2,1,0:T(8,128)(2,1)S(1)}, bf16...) custom-call(bf16[256,512]{1,0:T(8,128)(2,1)} %x_in.1, ...), custom_call_target="tpu_custom_call" | custom-call | tf_op jit(solution)/shard_map/pallas_call | solution.py:411
  49.4 11.1 %shard_map.194 = (bf16[256,512]{1,0:T(8,128)(2,1)}, bf16[2,32,8,64,256]{4,3,2,1,0:T(8,128)(2,1)}, bf16[2,32,8,64,256]{4,3,2,1,0:T(8,128)(2,1)}) custom-call(bf16[32,8,64,256]{3,2,1,0:T(8,128)(2,1)S(1)} %get-tuple-element.22.ko0, bf16[32,8,64,256]{3,2,1,0:T(8,128)(2,1)S(1)} %get-tuple-element.23.vo0, bf16[32,8,64,256]{3,2,1,0:T(8,128)(2,1)S(1)} %get-tuple-element.24.ko1, ...), custom_call_target="tpu_custom_call" | custom-call | tf_op jit(solution)/shard_map/pallas_call | solution.py:440

commit v3 on v2

--- a/solution.py
+++ b/solution.py
@@ -66,6 +66,7 @@
 VEC = len(PIECES) - 1
 N_VEC = 10
 ITEMS = [item for piece in PIECES for item in piece]
+KEYS = list(dict.fromkeys(item[:2] for item in ITEMS))
 FIRST = [sum(len(piece) for piece in PIECES[:p]) for p in range(len(PIECES) + 1)]
 
 
@@ -152,7 +153,22 @@
             copy.start()
     pl.semaphore_wait(barrier, len(peers) + 1)
 
-    sends = {}
+    started = []
+
+    def remote(ref, key, stage, peer):
+        k = KEYS.index(key)
+        return pltpu.make_async_remote_copy(
+            src_ref=ref, dst_ref=ref, send_sem=send_sem.at[k, stage],
+            recv_sem=recv_sem.at[k, stage], device_id=(peer,), device_id_type=MESH)
+
+    def parts(key, stage):
+        at = ([pz, py, px], [pz, py, ALL], [pz, ALL, ALL])[min(stage, 2)]
+        return remote(whole(*key).at[(*at, core)], key, stage, peer_core)
+
+    def landed(p, stage):
+        for key in keys(p):
+            parts(key, stage).wait_recv()
+            yield from (i for i in ids(p) if ITEMS[i][:2] == key)
 
     def send(i, stage):
         m, l, r0, rn, c0, cn, o = ITEMS[i]
@@ -164,46 +180,39 @@
             at[2 - axes[2]] = 1 - place[axes[2]]
         ref = whole(m, l).at[(*at, core, pl.ds(r0, rn), pl.ds(c0, cn))]
         peer = peers[axes[stage]] if stage < 3 else peer_core
-        copy = pltpu.make_async_remote_copy(
-            src_ref=ref, dst_ref=ref, send_sem=send_sem.at[i, stage],
-            recv_sem=recv_sem.at[i, stage], device_id=(peer,), device_id_type=MESH)
-        copy.start()
-        sends[(i, stage)] = copy
+        remote(ref, (m, l), stage, peer).start()
+        if ((m, l), stage) not in started:
+            started.append(((m, l), stage))
 
     def ids(p):
         return range(FIRST[p], FIRST[p + 1])
 
-    waited = set()
+    def keys(p):
+        return list(dict.fromkeys(ITEMS[i][:2] for i in ids(p)))
 
     def a(p):
-        for i in ids(p):
-            key = ITEMS[i][:2]
-            if key in local and key not in waited:
-                waited.add(key)
+        for key in keys(p):
+            if key in local:
                 local[key].wait()
         for i in ids(p):
             send(i, 0)
 
     def b(p):
-        for i in ids(p):
-            sends[(i, 0)].wait_recv()
+        for i in landed(p, 0):
             send(i, 1)
 
     def c(p):
-        for i in ids(p):
-            sends[(i, 1)].wait_recv()
+        for i in landed(p, 1):
             send(i, 2)
             send(i, 3)
 
     def d(p):
-        for i in ids(p):
-            sends[(i, 2)].wait_recv()
+        for i in landed(p, 2):
             send(i, 4)
 
     def e(p):
-        for i in ids(p):
-            sends[(i, 3)].wait_recv()
-            sends[(i, 4)].wait_recv()
+        for stage in (3, 4):
+            list(landed(p, stage))
 
     a(0)
     for copy in small[:N_VEC]:
@@ -337,8 +346,8 @@
     e(4)
     d(5)
     e(5)
-    for copy in sends.values():
-        copy.wait_send()
+    for key, stage in started:
+        parts(key, stage).wait_send()
 
 
 def finish_kernel(ko0, vo0, ko1, vo1, wo1, wi1, wd1, qs, kn, vn, ctxt, hcur, h2s, lnp, bin_, pos_ref,
@@ -428,8 +437,8 @@
                 pltpu.SemaphoreType.DMA((8,)),
                 pltpu.SemaphoreType.DMA((4,)),
                 pltpu.SemaphoreType.DMA((2 + N_VEC,)),
-                pltpu.SemaphoreType.DMA((len(ITEMS), 5)),
-                pltpu.SemaphoreType.DMA((len(ITEMS), 5)),
+                pltpu.SemaphoreType.DMA((len(KEYS), 5)),
+                pltpu.SemaphoreType.DMA((len(KEYS), 5)),
                 *[pltpu.VMEM(array.shape, BF16) for array in vectors],
             ],
             compiler_params=pltpu.CompilerParams(

time: 60.6 us -> 59.9 us (0.988)
  Pallas kernels: 59.8 us -> 59.1 us
    pallas_call x1, Pallas kernels: 48.8 us -> 48.1 us  [device_step(): pl.pallas_call(gather_kernel, out_shape=carried, in_specs=[hbm] * (8 + N_...]
where the time goes in v3:
time: 59.9 us; the launch traced here: 59.8 us
  Pallas kernels  59.1 us (99%)
  between operations  0.65 us (1%)
    pallas_call x1, Pallas kernels, device_step(): pl.pallas_call(gather_kernel, out_shape=carried, in_specs=[hbm] * (8 + N_...  48.1 us
    pallas_call x1, Pallas kernels, device_step(): pl.pallas_call(finish_kernel, out_shape=(pltpu.HBM((SEQS, WIDTH), BF16),...  11.1 us

profile of v3, /device:TPU:0, one launch (start us, length us, event | category | flops | bytes accessed | tf_op | source)
XLA Modules:
  0.0 59.8 jit_solution(513277644989679439)
XLA Ops:
  0.6 48.1 %shard_map.193 = (bf16[32,8,64,256]{3,2,1,0:T(8,128)(2,1)S(1)}, bf16[32,8,64,256]{3,2,1,0:T(8,128)(2,1)S(1)}, bf16[32,8,64,256]{3,2,1,0:T(8,128)(2,1)S(1)}, bf16...) custom-call(bf16[256,512]{1,0:T(8,128)(2,1)} %x_in.1, ...), custom_call_target="tpu_custom_call" | custom-call | tf_op jit(solution)/shard_map/pallas_call | solution.py:420
  48.7 11.1 %shard_map.194 = (bf16[256,512]{1,0:T(8,128)(2,1)}, bf16[2,32,8,64,256]{4,3,2,1,0:T(8,128)(2,1)}, bf16[2,32,8,64,256]{4,3,2,1,0:T(8,128)(2,1)}) custom-call(bf16[32,8,64,256]{3,2,1,0:T(8,128)(2,1)S(1)} %get-tuple-element.22.ko0, bf16[32,8,64,256]{3,2,1,0:T(8,128)(2,1)S(1)} %get-tuple-element.23.vo0, bf16[32,8,64,256]{3,2,1,0:T(8,128)(2,1)S(1)} %get-tuple-element.24.ko1, ...), custom_call_target="tpu_custom_call" | custom-call | tf_op jit(solution)/shard_map/pallas_call | solution.py:449

commit v4 on v3

--- a/solution.py
+++ b/solution.py
@@ -15,7 +15,7 @@
 PAIR = 6 * HEAD
 EARLY = 2
 ALL = slice(None)
-SCOPED = 20 * 2 ** 20
+SCOPED = 19 * 2 ** 20
 
 ERF_NUM = (-2.72614225801306e-10, 2.77068142495902e-08, -2.10102402082508e-06,
            -5.69250639462346e-05, -7.34990630326855e-04, -2.95459980854025e-03,
@@ -52,17 +52,18 @@
     return lax.broadcasted_iota(jnp.int32, shape, axis)
 
 
+QKV = 3 * WIDTH
+WEIGHTS = 3
+
+
 def pieces(l):
-    rows = (l, 0, SLOTS)
     third = 5 * LANES
-    qo = [(0, *rows, 0, third, 0), (0, *rows, third, third, 1),
-          (0, *rows, 2 * third, 2 * LANES, 2), (1, *rows, 0, WIDTH, 2)]
-    up = [(2, *rows, 0, third, 0), (2, *rows, third, third, 1), (2, *rows, 2 * third, 6 * LANES, 2)]
-    down = [(3, l, 0, 48, 0, WIDTH, 0), (3, l, 48, 48, 0, WIDTH, 1), (3, l, 96, SLOTS, 0, WIDTH, 2)]
-    return [qo, up, down]
-
-
-PIECES = pieces(0) + pieces(1) + [[(4, 0, 0, HEADS, 0, LANES, 0)]]
+    cols = ((0, third, 0), (third, third, 1), (2 * third, 6 * LANES, 2))
+    down = [(2, l, 0, 48, 0, WIDTH, 0), (2, l, 48, 48, 0, WIDTH, 1), (2, l, 96, SLOTS, 0, WIDTH, 2)]
+    return [[(m, l, 0, SLOTS, *c) for c in cols] for m in range(2)] + [down]
+
+
+PIECES = pieces(0) + pieces(1) + [[(WEIGHTS, 0, 0, HEADS, 0, LANES, 0)]]
 VEC = len(PIECES) - 1
 N_VEC = 10
 ITEMS = [item for piece in PIECES for item in piece]
@@ -100,9 +101,9 @@
     ctxt[h] = ctx.astype(BF16).astype(F32)
 
 
-def attn_out(ctxt, w, bias):
+def attn_out(ctxt, w_ref, bias):
     ctx = ctxt[...].reshape(WIDTH, SEQS).T.astype(BF16)
-    return dot(ctx, w.reshape(WIDTH, WIDTH)) + bias
+    return dot(ctx, w_ref[:, :, :, :, :, QKV:].reshape(WIDTH, WIDTH)) + bias
 
 
 def mlp_in(h, w_ref, bias_ref, l, act, n0, n1):
@@ -117,8 +118,8 @@
 
 
 def gather_body(x_in, pos_in, vec_in, wq_in, wo_in, wi_in, wd_in, kc_in, vc_in,
-                  ko0, vo0, ko1, vo1, wo1, wi1, wd1, qs, kn, vn, ctxt, hcur, h2s, lnp, bin_, pos_ref,
-                  wq, wo0, wi0, wd0, vecs, bqkv, sc, pr, act, accr, posb,
+                  ko0, vo0, ko1, vo1, wqo1, wi1, wd1, qs, kn, vn, ctxt, hcur, h2s, lnp, bin_, pos_ref,
+                  wqo0, wi0, wd0, vecs, bqkv, sc, pr, act, accr, posb,
                   local_sem, cache_sem, small_sem, send_sem, recv_sem, vec_ref):
     me = lax.axis_index('dp')
     core = me % 2
@@ -128,19 +129,22 @@
     place = (px, py, pz)
     peer_core = me + 1 - 2 * core
     peers = (me + 2 - 4 * px, me + 4 - 8 * py, me + 8 - 16 * pz)
-    shards = (wq_in, wo_in, wi_in, wd_in)
 
     def whole(m, l):
-        if m == 4:
+        if m == WEIGHTS:
             return vecs
-        return ((wq.at[0], wo0, wi0, wd0), (wq.at[1], wo1, wi1, wd1))[l][m]
-
-    local = {}
-    for l, m in [(l, m) for l in range(LAYERS) for m in range(4)]:
-        local[(m, l)] = pltpu.make_async_copy(
-            shards[m].at[l], whole(m, l).at[pz, py, px, core], local_sem.at[len(local)])
-    for m in range(2):
-        local[(m, 0)].start()
+        return ((wqo0, wi0, wd0), (wqo1, wi1, wd1))[l][m]
+
+    def place_own(m, l):
+        own = whole(m, l).at[pz, py, px, core]
+        sem = local_sem.at[m, l]
+        parts_in = [((wi_in, wd_in)[m - 1].at[l], own)]
+        if m == 0:
+            parts_in = [(wq_in.at[l], own.at[:, pl.ds(0, QKV)]), (wo_in.at[l], own.at[:, pl.ds(QKV, WIDTH)])]
+        for src, dst in parts_in:
+            pltpu.make_async_copy(src, dst, sem).start()
+
+    place_own(0, 0)
     barrier = pltpu.get_barrier_semaphore()
     for peer in peers + (peer_core,):
         pl.semaphore_signal(barrier, inc=1, device_id=(peer,), device_id_type=MESH)
@@ -148,21 +152,21 @@
     for src, dst in zip((*vec_in, pos_in, x_in), (*vec_ref, pos_ref, hcur)):
         small.append(pltpu.make_async_copy(src, dst, small_sem.at[len(small)]))
         small[-1].start()
-    for key, copy in local.items():
-        if key not in ((0, 0), (1, 0)):
-            copy.start()
+    for l in range(LAYERS):
+        for m in range(WEIGHTS):
+            if m + l:
+                place_own(m, l)
     pl.semaphore_wait(barrier, len(peers) + 1)
-
-    started = []
 
     def remote(ref, key, stage, peer):
         k = KEYS.index(key)
+        stage = min(stage, 3)
         return pltpu.make_async_remote_copy(
-            src_ref=ref, dst_ref=ref, send_sem=send_sem.at[k, stage],
+            src_ref=ref, dst_ref=ref, send_sem=send_sem.at[k // (LAYERS * WEIGHTS), stage],
             recv_sem=recv_sem.at[k, stage], device_id=(peer,), device_id_type=MESH)
 
     def parts(key, stage):
-        at = ([pz, py, px], [pz, py, ALL], [pz, ALL, ALL])[min(stage, 2)]
+        at = ([pz, py, px], [pz, py, ALL], [pz, ALL, ALL], [ALL] * 3)[stage]
         return remote(whole(*key).at[(*at, core)], key, stage, peer_core)
 
     def landed(p, stage):
@@ -181,8 +185,6 @@
         ref = whole(m, l).at[(*at, core, pl.ds(r0, rn), pl.ds(c0, cn))]
         peer = peers[axes[stage]] if stage < 3 else peer_core
         remote(ref, (m, l), stage, peer).start()
-        if ((m, l), stage) not in started:
-            started.append(((m, l), stage))
 
     def ids(p):
         return range(FIRST[p], FIRST[p + 1])
@@ -192,8 +194,10 @@
 
     def a(p):
         for key in keys(p):
-            if key in local:
-                local[key].wait()
+            m, l = key
+            if m < WEIGHTS:
+                own = whole(m, l).at[pz, py, px, core]
+                pltpu.make_async_copy(own, own, local_sem.at[m, l]).wait()
         for i in ids(p):
             send(i, 0)
 
@@ -211,8 +215,7 @@
             send(i, 4)
 
     def e(p):
-        for stage in (3, 4):
-            list(landed(p, stage))
+        list(landed(p, 3))
 
     a(0)
     for copy in small[:N_VEC]:
@@ -323,7 +326,7 @@
     heads(0, 4, 6)
     c(3)
     heads(0, 6, HEADS)
-    accr[...] = attn_out(ctxt, wo0[...], lnp[0, 4])
+    accr[...] = attn_out(ctxt, wqo0, lnp[0, 4])
     e(1)
     b(5)
     mlp_in(h2s, wi0, bin_, 0, act, 0, 4)
@@ -346,25 +349,27 @@
     e(4)
     d(5)
     e(5)
-    for key, stage in started:
-        parts(key, stage).wait_send()
-
-
-def finish_kernel(ko0, vo0, ko1, vo1, wo1, wi1, wd1, qs, kn, vn, ctxt, hcur, h2s, lnp, bin_, pos_ref,
+    for stage in range(4):
+        pages = ko0.at[pl.ds(0, WEIGHTS * 2 ** stage)]
+        remote(pages, KEYS[0], stage, peer_core).wait_send()
+        parts(KEYS[-1], stage).wait_send()
+
+
+def finish_kernel(ko0, vo0, ko1, vo1, wqo1, wi1, wd1, qs, kn, vn, ctxt, hcur, h2s, lnp, bin_, pos_ref,
                   out_hbm, k_hbm, v_hbm, kst, vst, ctxs, sc, pr, posb, act, outs, sems):
     last = LAYERS - 1
-    copies = []
-
-    def write(src, dst):
-        copies.append(pltpu.make_async_copy(src, dst, sems.at[len(copies)]))
-        copies[-1].start()
-
-    for src, dst in ((ko0, k_hbm), (vo0, v_hbm)):
+    outputs = (k_hbm, v_hbm, out_hbm)
+
+    def write(src, n, *at):
+        dst = outputs[n].at[at] if at else outputs[n]
+        pltpu.make_async_copy(src, dst, sems.at[n]).start()
+
+    for n, src in enumerate((ko0, vo0)):
         for g in range(2):
             part = pl.ds(g * (SLOTS // 2), SLOTS // 2)
-            write(src.at[part], dst.at[0, part])
-    for src, dst in ((ko1, k_hbm), (vo1, v_hbm)):
-        write(src.at[:, pl.ds(0, EARLY)], dst.at[last, :, pl.ds(0, EARLY)])
+            write(src.at[part], n, 0, part)
+    for n, src in enumerate((ko1, vo1)):
+        write(src.at[:, pl.ds(0, EARLY)], n, last, ALL, pl.ds(0, EARLY))
     pos = pos_ref[...]
     posb[...] = jnp.broadcast_to(pos.astype(F32), posb.shape).astype(BF16)
     ctxs[...] = ctxt[...]
@@ -378,16 +383,16 @@
         h = EARLY + i
         attend(h, pos, posb, qs, kn, vn, lambda s: ko1[s, h], lambda s: vo1[s, h],
                put(kst, i), put(vst, i), sc, pr, ctxs)
-        write(kst.at[i], k_hbm.at[last, :, h])
-        write(vst.at[i], v_hbm.at[last, :, h])
+        write(kst.at[i], 0, last, ALL, h)
+        write(vst.at[i], 1, last, ALL, h)
     mlp_in(h2s, wi1, bin_, last, act, 0, 8)
-    x = attn_out(ctxs, wo1[...], lnp[last, 4])
+    x = attn_out(ctxs, wqo1, lnp[last, 4])
     m = dot(act[...], wd1[...].reshape(FF, WIDTH)) + lnp[last, 5]
     x = (hcur[...].astype(F32) + x + m).astype(BF16).astype(F32)
     outs[...] = (normalize(x) * lnp[0, 6] + lnp[1, 6]).astype(BF16)
-    write(outs, out_hbm)
-    for copy in copies:
-        copy.wait()
+    write(outs, 2)
+    for n, ref in enumerate(outputs):
+        pltpu.make_async_copy(ref, ref, sems.at[n]).wait()
 
 
 def solution(mesh):
@@ -409,11 +414,10 @@
         hbm = pl.BlockSpec(memory_space=pl.ANY)
         cache_shape = (LAYERS, SLOTS, HEADS, HEAD, SEQS)
         head_shape = (HEADS, HEAD, SEQS)
-        out_w = GRID[1:] + (SLOTS, WIDTH)
         in_w = GRID[1:] + (SLOTS, FF)
         down_w = GRID[1:] + (LANES, WIDTH)
         carried = [pltpu.VMEM(shape, dtype) for shape, dtype in (
-            *[(cache_shape[1:], BF16)] * 4, (out_w, BF16), (in_w, BF16), (down_w, BF16),
+            *[(cache_shape[1:], BF16)] * 4, (in_w, BF16), (in_w, BF16), (down_w, BF16),
             (head_shape, F32), (head_shape, BF16), (head_shape, BF16), (head_shape, F32),
             ((SEQS, WIDTH), BF16), ((SEQS, WIDTH), BF16), ((LAYERS, 8, 1, WIDTH), F32),
             ((LAYERS, 8, 1, SEQS), F32), ((1, SEQS), jnp.int32))]
@@ -423,8 +427,7 @@
             in_specs=[hbm] * (8 + N_VEC),
             out_specs=[vmem] * len(carried),
             scratch_shapes=[
-                pltpu.VMEM(GRID + (SLOTS, 3 * WIDTH), BF16),
-                pltpu.VMEM(out_w, BF16),
+                pltpu.VMEM(in_w, BF16),
                 pltpu.VMEM(in_w, BF16),
                 pltpu.VMEM(down_w, BF16),
                 pltpu.VMEM(GRID[1:] + (8, LANES), BF16),
@@ -434,11 +437,11 @@
                 pltpu.VMEM((SEQS, FF), BF16),
                 pltpu.VMEM((SEQS, WIDTH), F32),
                 pltpu.VMEM((16, SEQS), BF16),
-                pltpu.SemaphoreType.DMA((8,)),
+                pltpu.SemaphoreType.DMA((WEIGHTS, LAYERS)),
                 pltpu.SemaphoreType.DMA((4,)),
                 pltpu.SemaphoreType.DMA((2 + N_VEC,)),
-                pltpu.SemaphoreType.DMA((len(KEYS), 5)),
-                pltpu.SemaphoreType.DMA((len(KEYS), 5)),
+                pltpu.SemaphoreType.DMA((LAYERS, 4)),
+                pltpu.SemaphoreType.DMA((len(KEYS), 4)),
                 *[pltpu.VMEM(array.shape, BF16) for array in vectors],
             ],
             compiler_params=pltpu.CompilerParams(
@@ -460,7 +463,7 @@
                 pltpu.VMEM((16, SEQS), BF16),
                 pltpu.VMEM((SEQS, FF), BF16),
                 pltpu.VMEM((SEQS, WIDTH), BF16),
-                pltpu.SemaphoreType.DMA((7 + 2 * (HEADS - EARLY),)),
+                pltpu.SemaphoreType.DMA((3,)),
             ],
             compiler_params=pltpu.CompilerParams(vmem_limit_bytes=SCOPED),
         )(*state)

time: 59.9 us -> 59.2 us (0.988)
  Pallas kernels: 59.1 us -> 58.4 us
where the time goes in v4:
time: 59.2 us; the launch traced here: 59.1 us
  Pallas kernels  58.4 us (99%)
  between operations  0.65 us (1%)
    pallas_call x1, Pallas kernels, device_step(): pl.pallas_call(gather_kernel, out_shape=carried, in_specs=[hbm] * (8 + N_...  47.5 us
    pallas_call x1, Pallas kernels, device_step(): pl.pallas_call(finish_kernel, out_shape=(pltpu.HBM((SEQS, WIDTH), BF16),...  10.9 us

profile of v4, /device:TPU:0, one launch (start us, length us, event | category | flops | bytes accessed | tf_op | source)
XLA Modules:
  0.0 59.1 jit_solution(7624740165875009851)
XLA Ops:
  0.6 47.5 %shard_map.193 = (bf16[32,8,64,256]{3,2,1,0:T(8,128)(2,1)S(1)}, bf16[32,8,64,256]{3,2,1,0:T(8,128)(2,1)S(1)}, bf16[32,8,64,256]{3,2,1,0:T(8,128)(2,1)S(1)}, bf16...) custom-call(bf16[256,512]{1,0:T(8,128)(2,1)} %x_in.1, ...), custom_call_target="tpu_custom_call" | custom-call | tf_op jit(solution)/shard_map/pallas_call | solution.py:424
  48.1 10.9 %shard_map.194 = (bf16[256,512]{1,0:T(8,128)(2,1)}, bf16[2,32,8,64,256]{4,3,2,1,0:T(8,128)(2,1)}, bf16[2,32,8,64,256]{4,3,2,1,0:T(8,128)(2,1)}) custom-call(bf16[32,8,64,256]{3,2,1,0:T(8,128)(2,1)S(1)} %get-tuple-element.22.ko0, bf16[32,8,64,256]{3,2,1,0:T(8,128)(2,1)S(1)} %get-tuple-element.23.vo0, bf16[32,8,64,256]{3,2,1,0:T(8,128)(2,1)S(1)} %get-tuple-element.24.ko1, ...), custom_call_target="tpu_custom_call" | custom-call | tf_op jit(solution)/shard_map/pallas_call | solution.py:452

commit v5 on v4

--- a/solution.py
+++ b/solution.py
@@ -32,9 +32,11 @@
 
 
 def gelu(v):
-    u = jnp.clip(v * (0.5 ** 0.5), -4.0, 4.0)
+    z = v * (0.5 ** 0.5)
+    u = jnp.clip(z, -4.0, 4.0)
     t = u * u
     erf = u * horner(ERF_NUM, t) / horner(ERF_DEN, t)
+    erf = jnp.where(z >= 4.0, 1.0, jnp.where(z <= -4.0, -1.0, erf))
     return 0.5 * v * (1.0 + erf)
 
 
@@ -156,6 +158,13 @@
         for m in range(WEIGHTS):
             if m + l:
                 place_own(m, l)
+    for copy in small[:N_VEC]:
+        copy.wait()
+    g1, b1, g2, b2, bo, bd, bq, bi, gf, bf = (ref[...].astype(F32) for ref in vec_ref)
+    pad = jnp.zeros((LAYERS, 32), F32)
+    groups = ([g1, b1, g2, b2], [bo, bd, jnp.concatenate([gf, bf], axis=0), pad], [bq, pad])
+    rows = [jnp.concatenate(group, axis=1) for group in groups] + [bi]
+    vecs[pz, py, px, core] = jnp.concatenate(rows, axis=0).astype(BF16)
     pl.semaphore_wait(barrier, len(peers) + 1)
 
     def remote(ref, key, stage, peer):
@@ -218,13 +227,6 @@
         list(landed(p, 3))
 
     a(0)
-    for copy in small[:N_VEC]:
-        copy.wait()
-    g1, b1, g2, b2, bo, bd, bq, bi, gf, bf = (ref[...].astype(F32) for ref in vec_ref)
-    pad = jnp.zeros((LAYERS, 32), F32)
-    groups = ([g1, b1, g2, b2], [bo, bd, jnp.concatenate([gf, bf], axis=0), pad], [bq, pad])
-    rows = [jnp.concatenate(group, axis=1) for group in groups] + [bi]
-    vecs[pz, py, px, core] = jnp.concatenate(rows, axis=0).astype(BF16)
     a(VEC)
     a(1)
     a(2)

time: 59.2 us -> 59.2 us (level)
  no operation moved by 1% of the time
where the time goes in v5:
time: 59.2 us; the launch traced here: 59.1 us
  Pallas kernels  58.4 us (99%)
  between operations  0.65 us (1%)
    pallas_call x1, Pallas kernels, device_step(): pl.pallas_call(gather_kernel, out_shape=carried, in_specs=[hbm] * (8 + N_...  47.5 us
    pallas_call x1, Pallas kernels, device_step(): pl.pallas_call(finish_kernel, out_shape=(pltpu.HBM((SEQS, WIDTH), BF16),...  10.9 us

profile of v5, /device:TPU:0, one launch (start us, length us, event | category | flops | bytes accessed | tf_op | source)
XLA Modules:
  0.0 59.1 jit_solution(13894153116443656060)
XLA Ops:
  0.6 47.5 %shard_map.193 = (bf16[32,8,64,256]{3,2,1,0:T(8,128)(2,1)S(1)}, bf16[32,8,64,256]{3,2,1,0:T(8,128)(2,1)S(1)}, bf16[32,8,64,256]{3,2,1,0:T(8,128)(2,1)S(1)}, bf16...) custom-call(bf16[256,512]{1,0:T(8,128)(2,1)} %x_in.1, ...), custom_call_target="tpu_custom_call" | custom-call | tf_op jit(solution)/shard_map/pallas_call | solution.py:426
  48.1 10.9 %shard_map.194 = (bf16[256,512]{1,0:T(8,128)(2,1)}, bf16[2,32,8,64,256]{4,3,2,1,0:T(8,128)(2,1)}, bf16[2,32,8,64,256]{4,3,2,1,0:T(8,128)(2,1)}) custom-call(bf16[32,8,64,256]{3,2,1,0:T(8,128)(2,1)S(1)} %get-tuple-element.22.ko0, bf16[32,8,64,256]{3,2,1,0:T(8,128)(2,1)S(1)} %get-tuple-element.23.vo0, bf16[32,8,64,256]{3,2,1,0:T(8,128)(2,1)S(1)} %get-tuple-element.24.ko1, ...), custom_call_target="tpu_custom_call" | custom-call | tf_op jit(solution)/shard_map/pallas_call | solution.py:454

commit v6 on v5

--- a/solution.py
+++ b/solution.py
@@ -62,7 +62,8 @@
     third = 5 * LANES
     cols = ((0, third, 0), (third, third, 1), (2 * third, 6 * LANES, 2))
     down = [(2, l, 0, 48, 0, WIDTH, 0), (2, l, 48, 48, 0, WIDTH, 1), (2, l, 96, SLOTS, 0, WIDTH, 2)]
-    return [[(m, l, 0, SLOTS, *c) for c in cols] for m in range(2)] + [down]
+    qo, up = ([(m, l, 0, SLOTS, *c) for c in cols] for m in range(2))
+    return [qo, up, down] if l == 0 else [qo, down, up]
 
 
 PIECES = pieces(0) + pieces(1) + [[(WEIGHTS, 0, 0, HEADS, 0, LANES, 0)]]
@@ -348,8 +349,8 @@
     cache[3].wait()
     heads(1, 0, EARLY)
     d(4)
+    d(5)
     e(4)
-    d(5)
     e(5)
     for stage in range(4):
         pages = ko0.at[pl.ds(0, WEIGHTS * 2 ** stage)]

time: 59.2 us -> 59 us (level)
  no operation moved by 1% of the time
where the time goes in v6:
time: 59 us; the launch traced here: 58.8 us
  Pallas kernels  58.2 us (99%)
  between operations  0.65 us (1%)
    pallas_call x1, Pallas kernels, device_step(): pl.pallas_call(gather_kernel, out_shape=carried, in_specs=[hbm] * (8 + N_...  47.2 us
    pallas_call x1, Pallas kernels, device_step(): pl.pallas_call(finish_kernel, out_shape=(pltpu.HBM((SEQS, WIDTH), BF16),...  10.9 us

profile of v6, /device:TPU:0, one launch (start us, length us, event | category | flops | bytes accessed | tf_op | source)
XLA Modules:
  0.0 58.8 jit_solution(4433150584734694686)
XLA Ops:
  0.6 47.2 %shard_map.193 = (bf16[32,8,64,256]{3,2,1,0:T(8,128)(2,1)S(1)}, bf16[32,8,64,256]{3,2,1,0:T(8,128)(2,1)S(1)}, bf16[32,8,64,256]{3,2,1,0:T(8,128)(2,1)S(1)}, bf16...) custom-call(bf16[256,512]{1,0:T(8,128)(2,1)} %x_in.1, ...), custom_call_target="tpu_custom_call" | custom-call | tf_op jit(solution)/shard_map/pallas_call | solution.py:427
  47.9 10.9 %shard_map.194 = (bf16[256,512]{1,0:T(8,128)(2,1)}, bf16[2,32,8,64,256]{4,3,2,1,0:T(8,128)(2,1)}, bf16[2,32,8,64,256]{4,3,2,1,0:T(8,128)(2,1)}) custom-call(bf16[32,8,64,256]{3,2,1,0:T(8,128)(2,1)S(1)} %get-tuple-element.22.ko0, bf16[32,8,64,256]{3,2,1,0:T(8,128)(2,1)S(1)} %get-tuple-element.23.vo0, bf16[32,8,64,256]{3,2,1,0:T(8,128)(2,1)S(1)} %get-tuple-element.24.ko1, ...), custom_call_target="tpu_custom_call" | custom-call | tf_op jit(solution)/shard_map/pallas_call | solution.py:455

commit v7 on v6

--- a/solution.py
+++ b/solution.py
@@ -231,12 +231,13 @@
     a(VEC)
     a(1)
     a(2)
-    cache = []
     ko, vo = (ko0, ko1), (vo0, vo1)
     for l in range(LAYERS):
         for src, dst in ((kc_in, ko), (vc_in, vo)):
-            cache.append(pltpu.make_async_copy(src.at[l], dst[l], cache_sem.at[len(cache)]))
-            cache[-1].start()
+            pltpu.make_async_copy(src.at[l], dst[l], cache_sem.at[l]).start()
+
+    def cache_here(l):
+        pltpu.make_async_copy(kc_in, kc_in, cache_sem.at[l]).wait()
 
     for copy in small[N_VEC:]:
         copy.wait()
@@ -320,8 +321,7 @@
     e(0)
     c(2)
     qkv_stage(0)
-    cache[0].wait()
-    cache[1].wait()
+    cache_here(0)
     heads(0, 0, 4)
     a(5)
     b(4)
@@ -345,8 +345,7 @@
     c(5)
     e(3)
     qkv_stage(1)
-    cache[2].wait()
-    cache[3].wait()
+    cache_here(1)
     heads(1, 0, EARLY)
     d(4)
     d(5)
@@ -441,7 +440,7 @@
                 pltpu.VMEM((SEQS, WIDTH), F32),
                 pltpu.VMEM((16, SEQS), BF16),
                 pltpu.SemaphoreType.DMA((WEIGHTS, LAYERS)),
-                pltpu.SemaphoreType.DMA((4,)),
+                pltpu.SemaphoreType.DMA((LAYERS,)),
                 pltpu.SemaphoreType.DMA((2 + N_VEC,)),
                 pltpu.SemaphoreType.DMA((LAYERS, 4)),
                 pltpu.SemaphoreType.DMA((len(KEYS), 4)),

time: 59 us -> 58.9 us (level)
  no operation moved by 1% of the time
where the time goes in v7:
time: 58.9 us; the launch traced here: 58.8 us
  Pallas kernels  58.2 us (99%)
  between operations  0.65 us (1%)
    pallas_call x1, Pallas kernels, device_step(): pl.pallas_call(gather_kernel, out_shape=carried, in_specs=[hbm] * (8 + N_...  47.2 us
    pallas_call x1, Pallas kernels, device_step(): pl.pallas_call(finish_kernel, out_shape=(pltpu.HBM((SEQS, WIDTH), BF16),...  10.9 us

profile of v7, /device:TPU:0, one launch (start us, length us, event | category | flops | bytes accessed | tf_op | source)
XLA Modules:
  0.0 58.8 jit_solution(17306025990153765927)
XLA Ops:
  0.6 47.2 %shard_map.193 = (bf16[32,8,64,256]{3,2,1,0:T(8,128)(2,1)S(1)}, bf16[32,8,64,256]{3,2,1,0:T(8,128)(2,1)S(1)}, bf16[32,8,64,256]{3,2,1,0:T(8,128)(2,1)S(1)}, bf16...) custom-call(bf16[256,512]{1,0:T(8,128)(2,1)} %x_in.1, ...), custom_call_target="tpu_custom_call" | custom-call | tf_op jit(solution)/shard_map/pallas_call | solution.py:426
  47.9 10.9 %shard_map.194 = (bf16[256,512]{1,0:T(8,128)(2,1)}, bf16[2,32,8,64,256]{4,3,2,1,0:T(8,128)(2,1)}, bf16[2,32,8,64,256]{4,3,2,1,0:T(8,128)(2,1)}) custom-call(bf16[32,8,64,256]{3,2,1,0:T(8,128)(2,1)S(1)} %get-tuple-element.22.ko0, bf16[32,8,64,256]{3,2,1,0:T(8,128)(2,1)S(1)} %get-tuple-element.23.vo0, bf16[32,8,64,256]{3,2,1,0:T(8,128)(2,1)S(1)} %get-tuple-element.24.ko1, ...), custom_call_target="tpu_custom_call" | custom-call | tf_op jit(solution)/shard_map/pallas_call | solution.py:454
